TPU v7x, 256 devices: a whole 4x4x8 slice. The times are simulated.
256 devices in a mesh: dp: 32 (over x, z_lo, core), head: 8 (over y, z_hi).
Axes of the slice: x: 4, y: 4, z: 8 (z_hi: 2, z_lo: 4; z = z_hi * 4 + z_lo), core: 2. Of those that a mesh axis runs over, the one named last changes fastest.
Arguments:
- frames_in: bfloat16 [32, 8, 320, 640], P('dp', 'head'), may hold values from -6 to 6
- ln1_gain: float32 [1280], replicated, may hold values from 0.25 to 1.75
- ln1_bias: float32 [1280], replicated, may hold values from -3 to 3
- qkv_weight: bfloat16 [1280, 3, 1024], P('dp', None, 'head'), may hold values from -0.1875 to 0.1875
- qv_bias: float32 [2, 1024], P(None, 'head'), may hold values from -3 to 3
- out_weight: bfloat16 [1024, 1280], P(('head', 'dp')), may hold values from -0.1875 to 0.1875
- out_bias: float32 [1280], P('head'), may hold values from -3 to 3
- ln2_gain: float32 [1280], replicated, may hold values from 0.25 to 1.75
- ln2_bias: float32 [1280], replicated, may hold values from -3 to 3
- fc1_weight: bfloat16 [1280, 5120], P('dp', 'head'), may hold values from -0.15625 to 0.15625
- fc1_bias: float32 [5120], P('head'), may hold values from -3 to 3
- fc2_weight: bfloat16 [5120, 1280], P(('head', 'dp')), may hold values from -0.078125 to 0.078125
- fc2_bias: float32 [1280], P('head'), may hold values from -3 to 3
- server_of_clip: int32 [32], replicated, may hold values from 0 to 7
Outputs:
- encoded: bfloat16 [32, 8, 320, 640], P('dp', 'head')
All inputs are finite; a program needn't handle non-finite values.
Results may differ from a plain program's by a relative error of at most 0.014.
Values may be sent and summed in bfloat16 or wider, within the bound.
No kernel may reach another device: no remote copies, remote signals or barrier semaphores. Data moves between devices by JAX's collectives and lax.ppermute only.
A program may use at most 64 MiB of HBM per device.

v0:
```python
import jax
import jax.numpy as jnp
from jax import lax
from jax.sharding import Mesh
from jax.sharding import PartitionSpec as P

HDIM = 64
HEAD = ("head_0", "head_1")
HEAD_DP = ("head_0", "head_1", "dp")
epsilon = 1e-05


def laid_out(blocks, dim):
    dims = list(blocks.shape[1:])
    dims[dim] *= blocks.shape[0]
    return jnp.moveaxis(blocks, 0, dim).reshape(dims)


def sent_to_all(value, axis):
    copies = jnp.broadcast_to(value, (lax.axis_size(axis), *value.shape))
    return lax.all_to_all(copies, axis, split_axis=0, concat_axis=0, tiled=True)


def gather_directly(value, axis, dim):
    return laid_out(sent_to_all(value, axis), dim)


def own_rows(terms, axes):
    total = terms.astype(jnp.bfloat16)
    for axis in axes:
        total = lax.psum_scatter(total, axis, scatter_dimension=0, tiled=True)
    return total.astype(jnp.float32)


def layer_norm(matrix, gain_row, shift_row):
    floats = matrix.astype(jnp.float32)
    center = jnp.mean(floats, axis=-1, keepdims=True)
    spread = jnp.mean(jnp.square(floats - center), axis=-1, keepdims=True)
    return ((floats - center) * lax.rsqrt(spread + epsilon) * gain_row + shift_row).astype(
        jnp.bfloat16
    )


def normalize(residual_in, gain_row, shift_row):
    whole_rows = lax.all_gather(residual_in, HEAD, axis=1, tiled=True)
    return layer_norm(whole_rows, gain_row, shift_row)


def attend(queries, key_rows, value_rows):

    def single(triple):
        query_head, key_head, value_head = triple
        scores = jnp.dot(query_head, key_head.T, preferred_element_type=jnp.float32)
        maxima = jnp.max(scores, axis=-1, keepdims=True)
        weights = jnp.exp(scores - maxima)
        probability = (weights / jnp.sum(weights, axis=-1, keepdims=True)).astype(jnp.bfloat16)
        return jnp.dot(probability, value_head, preferred_element_type=jnp.float32).astype(
            jnp.bfloat16
        )

    per_head = lax.map(
        single,
        (jnp.swapaxes(queries, 0, 1), jnp.swapaxes(key_rows, 0, 1), jnp.swapaxes(value_rows, 0, 1)),
    )
    return jnp.swapaxes(per_head, 0, 1).reshape(queries.shape[0], -1)


def slot_order(server_list):
    clip_count = server_list.shape[0]
    indices = jnp.arange(clip_count, dtype=jnp.int32)
    earlier = (server_list[None, :] < server_list[:, None]) | (
        server_list[None, :] == server_list[:, None]
    ) & (indices[None, :] < indices[:, None])
    slot_of = jnp.sum(earlier.astype(jnp.int32), axis=1)
    return jnp.sum(jnp.where(slot_of[None, :] == indices[:, None], indices[None, :], 0), axis=1)


def regroup(block_rows, clip_order):
    group_size = lax.axis_size("dp")
    piece_rows = block_rows.reshape(group_size, -1)
    shuffled = lax.all_to_all(piece_rows, "dp", split_axis=0, concat_axis=0, tiled=True)
    picked = jnp.take(shuffled, clip_order, axis=0)
    returned = lax.all_to_all(picked, "dp", split_axis=0, concat_axis=0, tiled=True)
    return returned.reshape(block_rows.shape)


def block_term(operand, weight_rows, row_count, frame_count, local_width):
    blocks = row_count // frame_count
    product = jnp.dot(operand, weight_rows, preferred_element_type=jnp.float32)
    return (
        product.reshape(frame_count, blocks, local_width)
        .transpose(1, 0, 2)
        .reshape(blocks * frame_count, local_width)
    )


def on_device(
    frames_in,
    ln1_gain,
    ln1_bias,
    qkv_weight,
    qv_bias,
    out_weight,
    out_bias,
    ln2_gain,
    ln2_bias,
    fc1_weight,
    fc1_bias,
    fc2_weight,
    fc2_bias,
    server_of_clip,
):
    clip_order = slot_order(server_of_clip)
    group_rows = frames_in.shape[2]
    local_width = frames_in.shape[3] // 4
    frame_count = group_rows * 4
    residual_in = frames_in[0, 0].reshape(frame_count, local_width)
    residual_in = regroup(residual_in, clip_order)
    head_count = lax.axis_size(HEAD)
    normed_one = normalize(residual_in, ln1_gain, ln1_bias)
    column_count = qkv_weight.shape[2]
    weight_piece = lax.all_gather(qkv_weight, "dp", axis=0, tiled=True)
    operand = normed_one
    projected = jnp.dot(
        operand, weight_piece.reshape(weight_piece.shape[0], -1), preferred_element_type=jnp.float32
    ).reshape(frame_count, 3, column_count)
    queries = (
        ((projected[:, 0] + qv_bias[0]) * HDIM ** (-0.5))
        .astype(jnp.bfloat16)
        .reshape(frame_count, -1, HDIM)
    )
    key_rows = projected[:, 1].astype(jnp.bfloat16).reshape(frame_count, -1, HDIM)
    value_rows = (projected[:, 2] + qv_bias[1]).astype(jnp.bfloat16).reshape(frame_count, -1, HDIM)
    context = attend(queries, key_rows, value_rows)
    output_rows = lax.all_gather(out_weight, "dp", axis=0, tiled=True)
    carried = residual_in.astype(jnp.float32) + out_bias
    whole_context = gather_directly(context, HEAD, 1)
    split_rows = output_rows.reshape(output_rows.shape[0], head_count, local_width)
    feature_columns = lax.all_to_all(
        split_rows, HEAD, split_axis=1, concat_axis=0, tiled=True
    ).reshape(-1, local_width)
    attended = (
        carried + jnp.dot(whole_context, feature_columns, preferred_element_type=jnp.float32)
    ).astype(jnp.bfloat16)
    normed_two = normalize(attended, ln2_gain, ln2_bias)
    operand = normed_two
    hidden_sums = jnp.dot(
        operand, gather_directly(fc1_weight, "dp", 0), preferred_element_type=jnp.float32
    )
    hidden = jax.nn.gelu(hidden_sums + fc1_bias, approximate=False).astype(jnp.bfloat16)
    down_rows = lax.all_gather(fc2_weight, "dp", axis=0, tiled=True)
    kept = attended.astype(jnp.float32) + fc2_bias
    layer_out = (
        kept
        + own_rows(
            block_term(
                hidden, down_rows, frame_count * lax.axis_size(HEAD), frame_count, local_width
            ),
            HEAD,
        )
    ).astype(jnp.bfloat16)
    return layer_out.reshape(1, 1, group_rows, 4 * local_width)


def solution(mesh):
    torus = Mesh(mesh.devices.reshape(mesh.shape["dp"], 4, 2), ("dp", "head_0", "head_1"))
    return jax.shard_map(
        on_device,
        mesh=torus,
        in_specs=(
            P("dp", HEAD, None, None),
            P(),
            P(),
            P("dp", None, HEAD),
            P(None, HEAD),
            P(HEAD_DP, None),
            P(HEAD),
            P(),
            P(),
            P("dp", HEAD),
            P(HEAD),
            P(HEAD_DP, None),
            P(HEAD),
            P(),
        ),
        out_specs=P("dp", HEAD, None, None),
        check_vma=False,
    )
```

profile of v0, /device:TPU:2, one launch (start us, length us, event | category | flops | bytes accessed | tf_op | source)
XLA Modules:
  0.0 519.4 jit_solution(1292017763583869009)
XLA Ops:
  7.4 2.4 all_to_all.38
  10.3 3.1 reduce.9
  13.4 0.9 reshape.166
  14.3 9.1 %all-to-all-start = ((bf16[32,2,3200]{2,1,0:T(2,128)(2,1)}), bf16[32,2,3200]{2,1,0:T(2,128)(2,1)S(1)}, u32[]{:S(2)}, u32[]{:S(2)}) async-start(bf16[32,2,3200]{2,1,0:T(2,128)(2,1)} %reshape.166), calls=%async_computation | async-start | bytes 819200 | tf_op jit(solution)/shard_map/all_to_all | solution.py:81
  23.7 11.2 %all-to-all-done = bf16[32,2,3200]{2,1,0:T(2,128)(2,1)S(1)} async-done(((bf16[32,2,3200]{2,1,0:T(2,128)(2,1)}), bf16[32,2,3200]{2,1,0:T(2,128)(2,1)S(1)}, u32[]{:S(2)}, u32[]{:S(2)}) %all-to-all-start) | async-done | bytes 409632 | tf_op jit(solution)/shard_map/all_to_all | solution.py:81
  35.3 0.8 gather_fusion
  36.2 0.9 reduce.10
  37.2 17.8 %all_to_all.44 = bf16[32,2,3200]{2,1,0:T(2,128)(2,1)S(1)} all-to-all(bf16[32,2,3200]{2,1,0:T(2,128)(2,1)S(1)} %reshape.168), channel_id=1, replica_groups=mesh['dp'=32,'head_0'=4,'head_1'=2] {'dp'}, dimensions={0} | all-to-all | bytes 819200 | tf_op jit(solution)/shard_map/all_to_all | solution.py:83
  55.4 2.4 reduce
  57.8 0.8 reshape.131
  58.7 1.0 copy.56
  59.7 38.8 %all-gather = bf16[32,4,1280]{2,1,0:T(4,128)(2,1)S(1)} all-gather(bf16[1,4,1280]{2,1,0:T(4,128)(2,1)S(1)} %bitcast.96), channel_id=1, replica_groups=mesh['dp'=32,'head_0'=4,'head_1'=2] {'dp'}, dimensions={0}, use_global_device_ids=true | all-gather | bytes 337920 | tf_op jit(solution)/shard_map/all_gather | solution.py:135
  98.5 0.7 reshape.135
  99.2 1.1 copy.63
  100.3 7.2 %all-to-all-start.3 = ((bf16[128,8,160]{0,2,1:T(8,128)(2,1)}), bf16[128,8,160]{0,2,1:T(8,128)(2,1)S(1)}, u32[]{:S(2)}, u32[]{:S(2)}) async-start(bf16[128,8,160]{0,2,1:T(8,128)(2,1)} %copy.63), calls=%async_computation.3 | async-start | bytes 655360 | tf_op jit(solution)/shard_map/all_to_all | solution.py:139
  107.5 64.6 %all_gather.16 = bf16[1280,3,128]{2,0,1:T(8,128)(2,1)S(1)} all-gather(bf16[40,3,128]{2,0,1:T(8,128)(2,1)S(1)} %copy-done.8), channel_id=1, replica_groups=mesh['dp'=32,'head_0'=4,'head_1'=2] {'dp'}, dimensions={0}, use_global_device_ids=true | all-gather | bytes 1013760 | tf_op jit(solution)/shard_map/all_gather | solution.py:122
  172.9 2.6 convert_reduce_fusion.1
  175.8 0.9 fusion.22
  176.7 1.8 fusion.41
  179.1 1.5 copy.62
  180.9 2.4 fusion.50
  183.4 8.4 %while.10 = (s32[]{:T(128)}, bf16[2,1280,64]{1,2,0:T(8,128)(2,1)}, bf16[2,1280,64]{2,1,0:T(8,128)(2,1)S(1)}, bf16[2,1280,64]{2,1,0:T(8,128)(2,1)S(1)}, bf16[2,1280,64]{2,1,0:T(8,128)(2,1)}, /*index=5*/s32[]{:T(128)}) while((s32[]{:T(128)}, bf16[2,1280,64]{1,2,0:T(8,128)(2,1)}, bf16[2,1280,64]{2,1,0:T(8,128)(2,1)S(1)}, ...), condition=%wide.region_7.8_spmd, body=%wide.region_4.7_spmd.sunk | while | flops 429340160 | bytes 24773784 | solution.py:61
  183.4 1.0 fusion.97
  184.4 1.0 fusion.98
  185.6 1.3 fusion.99
  186.8 0.7 copy-done.6
  187.6 1.0 fusion.97
  188.6 1.0 fusion.98
  189.8 1.3 fusion.99
  191.0 0.7 copy-done.6
  191.8 2.6 broadcast_in_dim.36
  194.4 8.3 %all-to-all-start.2 = ((bf16[8,1280,128]{1,2,0:T(8,128)(2,1)}), bf16[8,1280,128]{1,2,0:T(8,128)(2,1)S(1)}, u32[]{:S(2)}, u32[]{:S(2)}) async-start(bf16[8,1280,128]{1,2,0:T(8,128)(2,1)} %broadcast_in_dim.36), calls=%async_computation.2 | async-start | bytes 5242880 | tf_op jit(solution)/shard_map/all_to_all | solution.py:21
  203.3 0.9 copy.64
  204.2 61.5 %all-to-all-done.2 = bf16[8,1280,128]{1,2,0:T(8,128)(2,1)S(1)} async-done(((bf16[8,1280,128]{1,2,0:T(8,128)(2,1)}), bf16[8,1280,128]{1,2,0:T(8,128)(2,1)S(1)}, u32[]{:S(2)}, u32[]{:S(2)}) %all-to-all-start.2) | async-done | bytes 2621472 | tf_op jit(solution)/shard_map/all_to_all | solution.py:21
  265.7 2.3 fusion.46
  268.0 1.4 broadcast_in_dim.37
  269.4 12.6 %all-to-all-start.4 = ((bf16[32,40,640]{2,1,0:T(8,128)(2,1)}), bf16[32,40,640]{2,1,0:T(8,128)(2,1)}, u32[]{:S(2)}, u32[]{:S(2)}) async-start(bf16[32,40,640]{2,1,0:T(8,128)(2,1)} %broadcast_in_dim.37), calls=%async_computation.4 | async-start | bytes 3276800 | tf_op jit(solution)/shard_map/all_to_all | solution.py:21
  282.1 31.7 %all-gather.10.cloned.1.call-done = bf16[32,20,1280]{2,1,0:T(8,128)(2,1)} async-done(((bf16[1,20,1280]{2,1,0:T(8,128)(2,1)}), bf16[32,20,1280]{2,1,0:T(8,128)(2,1)}) %all-gather.10.cloned.1.call-update) | async-done | bytes 1638416 | tf_op jit(solution)/shard_map/all_gather | solution.py:151
  313.8 4.1 reshape.150
  317.9 93.8 %all-gather.8.cloned.1.call-done = bf16[1280,1280]{0,1:T(8,128)(2,1)} async-done(((bf16[1280,160]{0,1:T(8,128)(2,1)}), bf16[1280,1280]{0,1:T(8,128)(2,1)}) %all-gather.8.cloned.1.call-update) | async-done | bytes 3276816 | tf_op jit(solution)/shard_map/all_gather | solution.py:45
  411.8 2.6 convert_reduce_fusion
  414.7 0.9 fusion.18
  415.6 15.6 %convolution_convert_fusion = bf16[1280,1280]{0,1:T(8,128)(2,1)} fusion(bf16[640,1280]{1,0:T(8,128)(2,1)} %reshape.150, bf16[1280,640]{1,0:T(8,128)(2,1)} %bitcast.24, bf16[1280,1280]{0,1:T(8,128)(2,1)S(1)} %copy-done.1, f32[1280]{0:T(1024)S(1)} %copy-done.15, f32[1280]{0:T(1024)S(1)} %copy-done.16, f32[1280]{0:T(1024)S(1)} %add_rsqrt_fusion, ...), kind=kOutput, calls=%fused_computation.25 | convolution fusion | flops 4259840000 | bytes 9853440 | tf_op jit(solution)/shard_map/dot_general | solution.py:89
  431.2 4.0 copy.71
  435.3 37.3 %reduce-scatter.3.cloned.1.call-done = bf16[2560,160]{0,1:T(8,128)(2,1)} async-done(((bf16[10240,160]{0,1:T(8,128)(2,1)}), bf16[2560,160]{0,1:T(8,128)(2,1)}) %reduce-scatter.3.cloned.1.call-update) | async-done | bytes 819216 | tf_op jit(solution)/shard_map/reduce_scatter | solution.py:31
  472.7 35.9 %reduce-scatter.5.cloned.1.call-done = bf16[1280,160]{0,1:T(8,128)(2,1)} async-done(((bf16[2560,160]{0,1:T(8,128)(2,1)}), bf16[1280,160]{0,1:T(8,128)(2,1)}) %reduce-scatter.5.cloned.1.call-update) | async-done | bytes 409616 | tf_op jit(solution)/shard_map/reduce_scatter | solution.py:31
  508.6 1.2 add_convert_fusion.1
  510.0 1.6 reshape.138
  (80 shorter events, 5.6 us)
Async XLA Ops:
  7.4 16.0 %copy-start.18 = (s32[32]{0:T(128)S(1)}, s32[32]{0:T(128)}, u32[]{:S(2)}) copy-start(s32[32]{0:T(128)} %param.29) | copy-start | bytes 388
  14.3 20.7 %all-to-all-start = ((bf16[32,2,3200]{2,1,0:T(2,128)(2,1)}), bf16[32,2,3200]{2,1,0:T(2,128)(2,1)S(1)}, u32[]{:S(2)}, u32[]{:S(2)}) async-start(bf16[32,2,3200]{2,1,0:T(2,128)(2,1)} %reshape.166), calls=%async_computation | async-start | bytes 819200 | tf_op jit(solution)/shard_map/all_to_all | solution.py:81
  23.3 149.6 %all-gather.6.cloned.1.call-start = ((), (), s32[]{:S(2)}) async-start(), calls=%async_computation.7 | async-start | bytes 3686400 | tf_op jit(solution)/shard_map/all_gather | solution.py:45
  37.1 22.6 %copy-start.9 = (bf16[4,1280]{1,0:T(4,128)(2,1)S(1)}, bf16[4,1280]{1,0:T(4,128)(2,1)}, u32[]{:S(2)}) copy-start(bf16[4,1280]{1,0:T(4,128)(2,1)} %param.21) | copy-start | bytes 30724
  55.4 52.1 %copy-start.8 = (bf16[40,3,128]{2,0,1:T(8,128)(2,1)S(1)}, bf16[40,3,128]{2,0,1:T(8,128)(2,1)}, u32[]{:S(2)}) copy-start(bf16[40,3,128]{2,0,1:T(8,128)(2,1)} %param.19) | copy-start | bytes 92164
  59.7 113.0 %copy-start.10 = (f32[2,128]{1,0:T(2,128)S(1)}, f32[2,128]{1,0:T(2,128)}, u32[]{:S(2)}) copy-start(f32[2,128]{1,0:T(2,128)} %param.20) | copy-start | bytes 3076
  100.3 91.5 %all-to-all-start.3 = ((bf16[128,8,160]{0,2,1:T(8,128)(2,1)}), bf16[128,8,160]{0,2,1:T(8,128)(2,1)S(1)}, u32[]{:S(2)}, u32[]{:S(2)}) async-start(bf16[128,8,160]{0,2,1:T(8,128)(2,1)} %copy.63), calls=%async_computation.3 | async-start | bytes 655360 | tf_op jit(solution)/shard_map/all_to_all | solution.py:139
  172.9 3.9 copy-start.13
  172.9 3.9 copy-start.14
  172.9 2.9 copy-start
  184.4 1.1 copy-start.4
  184.4 1.2 copy-start.5
  186.8 0.7 copy-start.6
  188.6 1.1 copy-start.4
  188.6 1.2 copy-start.5
  191.0 0.7 copy-start.6
  194.4 71.2 %copy-start.2 = (bf16[1280,160]{0,1:T(8,128)(2,1)S(1)}, bf16[1280,160]{0,1:T(8,128)(2,1)}, u32[]{:S(2)}) copy-start(bf16[1280,160]{0,1:T(8,128)(2,1)} %copy.56) | copy-start | bytes 1228804
  194.4 71.2 %copy-start.12 = (f32[160]{0:T(256)S(1)}, f32[160]{0:T(256)}, u32[]{:S(2)}) copy-start(f32[160]{0:T(256)} %param.22) | copy-start | bytes 1924
  194.4 71.2 %all-to-all-start.2 = ((bf16[8,1280,128]{1,2,0:T(8,128)(2,1)}), bf16[8,1280,128]{1,2,0:T(8,128)(2,1)S(1)}, u32[]{:S(2)}, u32[]{:S(2)}) async-start(bf16[8,1280,128]{1,2,0:T(8,128)(2,1)} %broadcast_in_dim.36), calls=%async_computation.2 | async-start | bytes 5242880 | tf_op jit(solution)/shard_map/all_to_all | solution.py:21
  202.7 65.3 %copy-start.7 = (bf16[40,640]{1,0:T(8,128)(2,1)S(1)}, bf16[40,640]{1,0:T(8,128)(2,1)}, u32[]{:S(2)}) copy-start(bf16[40,640]{1,0:T(8,128)(2,1)} %param.25) | copy-start | bytes 153604
  202.7 111.1 %all-gather.10.cloned.1.call-start = ((), (), s32[]{:S(2)}) async-start(), calls=%async_computation.11 | async-start | bytes 2027520 | tf_op jit(solution)/shard_map/all_gather | solution.py:151
  203.3 208.5 %all-gather.8.cloned.1.call-start = ((), (), s32[]{:S(2)}) async-start(), calls=%async_computation.8 | async-start | bytes 3686400 | tf_op jit(solution)/shard_map/all_gather | solution.py:45
  269.4 146.2 %all-to-all-start.4 = ((bf16[32,40,640]{2,1,0:T(8,128)(2,1)}), bf16[32,40,640]{2,1,0:T(8,128)(2,1)}, u32[]{:S(2)}, u32[]{:S(2)}) async-start(bf16[32,40,640]{2,1,0:T(8,128)(2,1)} %broadcast_in_dim.37), calls=%async_computation.4 | async-start | bytes 3276800 | tf_op jit(solution)/shard_map/all_to_all | solution.py:21
  282.0 190.6 %reduce-scatter.3.cloned.1.call-start = ((), (), s32[]{:S(2)}) async-start(), calls=%async_computation.9 | async-start | bytes 4096000 | tf_op jit(solution)/shard_map/reduce_scatter | solution.py:31
  317.9 97.7 %copy-start.15 = (f32[1280]{0:T(1024)S(1)}, f32[1280]{0:T(1024)}, u32[]{:S(2)}) copy-start(f32[1280]{0:T(1024)} %param.24) | copy-start | bytes 15364
  317.9 97.7 %copy-start.16 = (f32[1280]{0:T(1024)S(1)}, f32[1280]{0:T(1024)}, u32[]{:S(2)}) copy-start(f32[1280]{0:T(1024)} %param.23) | copy-start | bytes 15364
  317.9 97.7 %copy-start.17 = (f32[640]{0:T(1024)S(1)}, f32[640]{0:T(1024)}, u32[]{:S(2)}) copy-start(f32[640]{0:T(1024)} %param.26) | copy-start | bytes 7684
  411.8 2.9 copy-start.1
  435.2 73.3 %copy-start.3 = (bf16[1280,160]{0,1:T(8,128)(2,1)S(1)}, bf16[1280,160]{0,1:T(8,128)(2,1)}, u32[]{:S(2)}) copy-start(bf16[1280,160]{0,1:T(8,128)(2,1)} %fusion.46) | copy-start | bytes 1228804
  435.2 73.3 %copy-start.11 = (f32[160]{0:T(256)S(1)}, f32[160]{0:T(256)}, u32[]{:S(2)}) copy-start(f32[160]{0:T(256)} %param.28) | copy-start | bytes 1924
  435.3 73.3 %reduce-scatter.5.cloned.1.call-start = ((), (), s32[]{:S(2)}) async-start(), calls=%async_computation.10 | async-start | bytes 1228800 | tf_op jit(solution)/shard_map/reduce_scatter | solution.py:31
Sparse Core Ops, SparseCore 0:
  59.8 99.7 all-gather.5
  435.4 37.2 reduce-scatter.2
Sparse Core Ops, SparseCore 1:
  205.1 108.7 all-gather.9
  316.3 95.4 all-gather.7
  472.8 35.7 reduce-scatter.4
where the time goes:
time: 528 us; the launch traced here: 519 us
  waiting for transfers between devices  272 us (52%)
  blocking collectives  121 us (23%)
  starting transfers between devices  37.3 us (7%)
  local copies, waits for them, and re-layouts  29.5 us (6%)
  matrix products  24.3 us (5%)
  other arithmetic  19.4 us (4%)
  between operations  15.5 us (3%)
    all_gather x2, waiting for transfers between devices, normalize(): whole_rows = lax.all_gather(residual_in, HEAD, axis=1, tiled=True)  93.8 us
    reduce_scatter x2, waiting for transfers between devices, own_rows(): total = lax.psum_scatter(total, axis, scatter_dimension=0, tiled=True)  73.2 us
    all_gather x1, blocking collectives, on_device(): weight_piece = lax.all_gather(qkv_weight, 'dp', axis=0, tiled=True)  64.6 us
    all_to_all x2, waiting for transfers between devices, sent_to_all(): return lax.all_to_all(copies, axis, split_axis=0, concat_axis=0, tiled=True)  61.5 us
    all_gather x1, blocking collectives, on_device(): output_rows = lax.all_gather(out_weight, 'dp', axis=0, tiled=True)  38.8 us
    all_gather x1, waiting for transfers between devices, on_device(): down_rows = lax.all_gather(fc2_weight, 'dp', axis=0, tiled=True)  31.7 us
    all_to_all x2, starting transfers between devices, sent_to_all(): return lax.all_to_all(copies, axis, split_axis=0, concat_axis=0, tiled=True)  20.9 us
    all_to_all x1, blocking collectives, regroup(): lax.all_to_all(picked, 'dp', split_axis=0, concat_axis=0, tiled=True)  17.8 us
  transfers between devices with their start and end apart: 9, of which 6 were waited for; matrix products, arithmetic and copies ran while one was open for 6% of the time, Pallas kernels for 0%

commit v1 on v0

--- a/solution.py
+++ b/solution.py
@@ -42,7 +42,7 @@
 
 
 def normalize(residual_in, gain_row, shift_row):
-    whole_rows = lax.all_gather(residual_in, HEAD, axis=1, tiled=True)
+    whole_rows = jnp.concatenate(lax.all_gather(residual_in, HEAD), axis=1)
     return layer_norm(whole_rows, gain_row, shift_row)
 
 

time: 528 us -> 533 us (level)
  waiting for transfers between devices: 272 us -> 261 us
  local copies, waits for them, and re-layouts: 29.5 us -> 36.6 us
  other arithmetic: 19.4 us -> 25.8 us
    all_to_all x2, waiting for transfers between devices: 61.5 us -> 51.3 us  [sent_to_all(): return lax.all_to_all(copies, axis, split_axis=0, concat_axis=0, tiled=True)]
    convert_element_type x0 -> x4, other arithmetic: none -> 6.49 us  [the longest x1 3.16 us: on_device(): carried = residual_in.astype(jnp.float32) + out_bias]
  transfers between devices with their start and end apart: 9 -> 9, of which waited for: 6 -> 6; matrix products, arithmetic and copies ran while one was open for 6% -> 9% of each run, Pallas kernels for 0% -> 0%
where the time goes in v1:
time: 533 us; the launch traced here: 525 us
  waiting for transfers between devices  261 us (49%)
  blocking collectives  123 us (23%)
  starting transfers between devices  38.8 us (7%)
  local copies, waits for them, and re-layouts  36.6 us (7%)
  other arithmetic  25.8 us (5%)
  matrix products  23.7 us (4%)
  between operations  15.8 us (3%)
    all_gather x2, waiting for transfers between devices, normalize(): whole_rows = jnp.concatenate(lax.all_gather(residual_in, HEAD), axis=1)  94.7 us
    reduce_scatter x2, waiting for transfers between devices, own_rows(): total = lax.psum_scatter(total, axis, scatter_dimension=0, tiled=True)  73.1 us
    all_gather x1, blocking collectives, on_device(): weight_piece = lax.all_gather(qkv_weight, 'dp', axis=0, tiled=True)  66.7 us
    all_to_all x2, waiting for transfers between devices, sent_to_all(): return lax.all_to_all(copies, axis, split_axis=0, concat_axis=0, tiled=True)  51.3 us
    all_gather x1, blocking collectives, on_device(): output_rows = lax.all_gather(out_weight, 'dp', axis=0, tiled=True)  38.8 us
    all_gather x1, waiting for transfers between devices, on_device(): down_rows = lax.all_gather(fc2_weight, 'dp', axis=0, tiled=True)  29.8 us
    all_to_all x2, starting transfers between devices, sent_to_all(): return lax.all_to_all(copies, axis, split_axis=0, concat_axis=0, tiled=True)  22.4 us
    all_to_all x1, blocking collectives, regroup(): lax.all_to_all(picked, 'dp', split_axis=0, concat_axis=0, tiled=True)  17.8 us
  transfers between devices with their start and end apart: 9, of which 6 were waited for; matrix products, arithmetic and copies ran while one was open for 9% of the time, Pallas kernels for 0%

profile of v1, /device:TPU:2, one launch (start us, length us, event | category | flops | bytes accessed | tf_op | source)
XLA Modules:
  0.0 524.7 jit_solution(17536133072313232044)
XLA Ops:
  7.4 2.4 all_to_all.38
  10.4 3.1 reduce.22
  13.5 0.9 reshape.227
  14.3 9.1 %all-to-all-start = ((bf16[32,2,3200]{2,1,0:T(2,128)(2,1)}), bf16[32,2,3200]{2,1,0:T(2,128)(2,1)S(1)}, u32[]{:S(2)}, u32[]{:S(2)}) async-start(bf16[32,2,3200]{2,1,0:T(2,128)(2,1)} %reshape.227), calls=%async_computation | async-start | bytes 819200 | tf_op jit(solution)/shard_map/all_to_all | solution.py:81
  23.8 11.2 %all-to-all-done = bf16[32,2,3200]{2,1,0:T(2,128)(2,1)S(1)} async-done(((bf16[32,2,3200]{2,1,0:T(2,128)(2,1)}), bf16[32,2,3200]{2,1,0:T(2,128)(2,1)S(1)}, u32[]{:S(2)}, u32[]{:S(2)}) %all-to-all-start) | async-done | bytes 409632 | tf_op jit(solution)/shard_map/all_to_all | solution.py:81
  36.3 0.9 reduce.23
  37.4 17.8 %all_to_all.44 = bf16[32,2,3200]{2,1,0:T(2,128)(2,1)S(1)} all-to-all(bf16[32,2,3200]{2,1,0:T(2,128)(2,1)S(1)} %reshape.229), channel_id=1, replica_groups=mesh['dp'=32,'head_0'=4,'head_1'=2] {'dp'}, dimensions={0} | all-to-all | bytes 819200 | tf_op jit(solution)/shard_map/all_to_all | solution.py:83
  55.6 2.4 reduce.11
  58.8 1.0 copy.62
  59.8 38.8 %all-gather.1 = bf16[32,4,1280]{2,1,0:T(4,128)(2,1)S(1)} all-gather(bf16[1,4,1280]{2,1,0:T(4,128)(2,1)S(1)} %bitcast.113), channel_id=1, replica_groups=mesh['dp'=32,'head_0'=4,'head_1'=2] {'dp'}, dimensions={0}, use_global_device_ids=true | all-gather | bytes 337920 | tf_op jit(solution)/shard_map/all_gather | solution.py:135
  99.3 1.1 copy.68
  100.4 7.2 %all-to-all-start.3 = ((bf16[128,8,160]{0,2,1:T(8,128)(2,1)}), bf16[128,8,160]{0,2,1:T(8,128)(2,1)}, u32[]{:S(2)}, u32[]{:S(2)}) async-start(bf16[128,8,160]{0,2,1:T(8,128)(2,1)} %copy.68), calls=%async_computation.3 | async-start | bytes 655360 | tf_op jit(solution)/shard_map/all_to_all | solution.py:139
  107.8 66.7 %all_gather.19 = bf16[1280,3,128]{2,0,1:T(8,128)(2,1)S(1)} all-gather(bf16[40,3,128]{2,0,1:T(8,128)(2,1)S(1)} %copy-done.7), channel_id=1, replica_groups=mesh['dp'=32,'head_0'=4,'head_1'=2] {'dp'}, dimensions={0}, use_global_device_ids=true | all-gather | bytes 1013760 | tf_op jit(solution)/shard_map/all_gather | solution.py:122
  175.3 2.6 convert_reduce_fusion
  178.2 0.9 fusion.16
  179.1 1.3 fusion.19
  180.5 1.5 fusion.31
  183.3 1.5 copy.67
  184.7 1.3 copy.66
  186.0 2.4 fusion.33
  188.4 8.4 %while.10 = (s32[]{:T(128)}, bf16[2,1280,64]{1,2,0:T(8,128)(2,1)}, bf16[2,1280,64]{2,1,0:T(8,128)(2,1)S(1)}, bf16[2,1280,64]{2,1,0:T(8,128)(2,1)S(1)}, bf16[2,1280,64]{2,1,0:T(8,128)(2,1)}, /*index=5*/s32[]{:T(128)}) while((s32[]{:T(128)}, bf16[2,1280,64]{1,2,0:T(8,128)(2,1)}, bf16[2,1280,64]{2,1,0:T(8,128)(2,1)S(1)}, ...), condition=%wide.region_7.8_spmd, body=%wide.region_4.7_spmd.sunk | while | flops 429340160 | bytes 24773784 | solution.py:61
  188.4 1.0 fusion.82
  189.5 1.0 fusion.83
  190.7 1.3 fusion.84
  192.6 1.0 fusion.82
  193.7 1.0 fusion.83
  194.8 1.3 fusion.84
  196.8 2.6 broadcast_in_dim.36
  199.5 7.9 %all-to-all-start.2 = ((bf16[8,1280,128]{1,2,0:T(8,128)(2,1)}), bf16[8,1280,128]{1,2,0:T(8,128)(2,1)S(1)}, u32[]{:S(2)}, u32[]{:S(2)}) async-start(bf16[8,1280,128]{1,2,0:T(8,128)(2,1)} %broadcast_in_dim.36), calls=%async_computation.2 | async-start | bytes 5242880 | tf_op jit(solution)/shard_map/all_to_all | solution.py:21
  208.0 1.8 copy.69
  209.8 3.2 convert_reduce_fusion.2
  213.0 3.0 reshape.195
  216.0 1.7 copy.61
  217.6 51.3 %all-to-all-done.2 = bf16[8,1280,128]{1,2,0:T(8,128)(2,1)S(1)} async-done(((bf16[8,1280,128]{1,2,0:T(8,128)(2,1)}), bf16[8,1280,128]{1,2,0:T(8,128)(2,1)S(1)}, u32[]{:S(2)}, u32[]{:S(2)}) %all-to-all-start.2) | async-done | bytes 2621472 | tf_op jit(solution)/shard_map/all_to_all | solution.py:21
  269.0 2.3 fusion.30
  271.4 1.3 broadcast_in_dim.37
  272.7 14.5 %all-to-all-start.4 = ((bf16[32,40,640]{2,1,0:T(8,128)(2,1)}), bf16[32,40,640]{2,1,0:T(8,128)(2,1)}, u32[]{:S(2)}, u32[]{:S(2)}) async-start(bf16[32,40,640]{2,1,0:T(8,128)(2,1)} %broadcast_in_dim.37), calls=%async_computation.4 | async-start | bytes 3276800 | tf_op jit(solution)/shard_map/all_to_all | solution.py:21
  287.4 29.8 %all-gather.11.cloned.1.call-done = bf16[32,20,1280]{2,1,0:T(8,128)(2,1)} async-done(((bf16[1,20,1280]{2,1,0:T(8,128)(2,1)}), bf16[32,20,1280]{2,1,0:T(8,128)(2,1)}) %all-gather.11.cloned.1.call-update) | async-done | bytes 1638416 | tf_op jit(solution)/shard_map/all_gather | solution.py:151
  317.1 3.6 reshape.210
  320.8 94.7 %all-gather.9.cloned.1.call-done = bf16[10240,160]{0,1:T(8,128)(2,1)} async-done(((bf16[1280,160]{0,1:T(8,128)(2,1)}), bf16[10240,160]{0,1:T(8,128)(2,1)}) %all-gather.9.cloned.1.call-update) | async-done | bytes 3276816 | tf_op jit(solution)/shard_map/all_gather | solution.py:45
  415.5 2.6 convert_reduce_fusion.1
  419.9 1.3 add_convert_fusion
  421.2 15.3 %convolution_convert_fusion = bf16[1280,1280]{0,1:T(8,128)(2,1)} fusion(bf16[640,1280]{1,0:T(8,128)(2,1)} %reshape.210, bf16[1280,1280]{0,1:T(8,128)(2,1)S(1)} %bitcast.104, bf16[1280,640]{1,0:T(8,128)(2,1)} %bitcast.28, f32[640]{0:T(1024)S(1)} %copy-done.16), kind=kOutput, calls=%fused_computation.21 | convolution fusion | flops 4250009600 | bytes 9832960 | tf_op jit(solution)/shard_map/dot_general | solution.py:89
  436.5 4.0 copy.78
  440.6 37.2 %reduce-scatter.3.cloned.1.call-done = bf16[2560,160]{0,1:T(8,128)(2,1)} async-done(((bf16[10240,160]{0,1:T(8,128)(2,1)}), bf16[2560,160]{0,1:T(8,128)(2,1)}) %reduce-scatter.3.cloned.1.call-update) | async-done | bytes 819216 | tf_op jit(solution)/shard_map/reduce_scatter | solution.py:31
  477.8 35.8 %reduce-scatter.5.cloned.1.call-done = bf16[1280,160]{0,1:T(8,128)(2,1)} async-done(((bf16[2560,160]{0,1:T(8,128)(2,1)}), bf16[1280,160]{0,1:T(8,128)(2,1)}) %reduce-scatter.5.cloned.1.call-update) | async-done | bytes 409616 | tf_op jit(solution)/shard_map/reduce_scatter | solution.py:31
  513.7 1.2 add_convert_fusion.2
  515.1 1.6 reshape.194
  (90 shorter events, 11.4 us)
Async XLA Ops:
  7.4 16.1 %copy-start.17 = (s32[32]{0:T(128)S(1)}, s32[32]{0:T(128)}, u32[]{:S(2)}) copy-start(s32[32]{0:T(128)} %param.29) | copy-start | bytes 388
  14.3 20.7 %all-to-all-start = ((bf16[32,2,3200]{2,1,0:T(2,128)(2,1)}), bf16[32,2,3200]{2,1,0:T(2,128)(2,1)S(1)}, u32[]{:S(2)}, u32[]{:S(2)}) async-start(bf16[32,2,3200]{2,1,0:T(2,128)(2,1)} %reshape.227), calls=%async_computation | async-start | bytes 819200 | tf_op jit(solution)/shard_map/all_to_all | solution.py:81
  23.4 151.9 %all-gather.7.cloned.1.call-start = ((), (), s32[]{:S(2)}) async-start(), calls=%async_computation.7 | async-start | bytes 3686400 | tf_op jit(solution)/shard_map/all_gather | solution.py:45
  37.3 22.6 %copy-start.8 = (bf16[4,1280]{1,0:T(4,128)(2,1)S(1)}, bf16[4,1280]{1,0:T(4,128)(2,1)}, u32[]{:S(2)}) copy-start(bf16[4,1280]{1,0:T(4,128)(2,1)} %param.21) | copy-start | bytes 30724
  55.5 52.1 %copy-start.9 = (f32[1280]{0:T(1024)S(1)}, f32[1280]{0:T(1024)}, u32[]{:S(2)}) copy-start(f32[1280]{0:T(1024)} %param.18) | copy-start | bytes 15364
  55.5 52.2 %copy-start.10 = (f32[1280]{0:T(1024)S(1)}, f32[1280]{0:T(1024)}, u32[]{:S(2)}) copy-start(f32[1280]{0:T(1024)} %param.17) | copy-start | bytes 15364
  55.5 52.3 %copy-start.7 = (bf16[40,3,128]{2,0,1:T(8,128)(2,1)S(1)}, bf16[40,3,128]{2,0,1:T(8,128)(2,1)}, u32[]{:S(2)}) copy-start(bf16[40,3,128]{2,0,1:T(8,128)(2,1)} %param.19) | copy-start | bytes 92164
  59.8 115.3 %copy-start.14 = (f32[2,128]{1,0:T(2,128)S(1)}, f32[2,128]{1,0:T(2,128)}, u32[]{:S(2)}) copy-start(f32[2,128]{1,0:T(2,128)} %param.20) | copy-start | bytes 3076
  100.4 96.4 %all-to-all-start.3 = ((bf16[128,8,160]{0,2,1:T(8,128)(2,1)}), bf16[128,8,160]{0,2,1:T(8,128)(2,1)}, u32[]{:S(2)}, u32[]{:S(2)}) async-start(bf16[128,8,160]{0,2,1:T(8,128)(2,1)} %copy.68), calls=%async_computation.3 | async-start | bytes 655360 | tf_op jit(solution)/shard_map/all_to_all | solution.py:139
  175.3 2.9 copy-start
  189.5 1.1 copy-start.3
  189.5 1.2 copy-start.4
  191.9 0.7 copy-start.5
  193.7 1.1 copy-start.3
  193.7 1.2 copy-start.4
  196.1 0.7 copy-start.5
  199.5 69.5 %all-to-all-start.2 = ((bf16[8,1280,128]{1,2,0:T(8,128)(2,1)}), bf16[8,1280,128]{1,2,0:T(8,128)(2,1)S(1)}, u32[]{:S(2)}, u32[]{:S(2)}) async-start(bf16[8,1280,128]{1,2,0:T(8,128)(2,1)} %broadcast_in_dim.36), calls=%async_computation.2 | async-start | bytes 5242880 | tf_op jit(solution)/shard_map/all_to_all | solution.py:21
  207.4 109.8 %all-gather.11.cloned.1.call-start = ((), (), s32[]{:S(2)}) async-start(), calls=%async_computation.11 | async-start | bytes 2027520 | tf_op jit(solution)/shard_map/all_gather | solution.py:151
  207.9 207.5 %all-gather.9.cloned.1.call-start = ((), (), s32[]{:S(2)}) async-start(), calls=%async_computation.10 | async-start | bytes 3686400 | tf_op jit(solution)/shard_map/all_gather | solution.py:45
  208.0 61.0 %copy-start.13 = (f32[160]{0:T(256)S(1)}, f32[160]{0:T(256)}, u32[]{:S(2)}) copy-start(f32[160]{0:T(256)} %param.22) | copy-start | bytes 1924
  216.0 55.4 %copy-start.6 = (bf16[40,640]{1,0:T(8,128)(2,1)S(1)}, bf16[40,640]{1,0:T(8,128)(2,1)}, u32[]{:S(2)}) copy-start(bf16[40,640]{1,0:T(8,128)(2,1)} %param.25) | copy-start | bytes 153604
  271.3 15.9 %copy-start.11 = (f32[1280]{0:T(1024)S(1)}, f32[1280]{0:T(1024)}, u32[]{:S(2)}) copy-start(f32[1280]{0:T(1024)} %param.24) | copy-start | bytes 15364
  271.3 16.0 %copy-start.12 = (f32[1280]{0:T(1024)S(1)}, f32[1280]{0:T(1024)}, u32[]{:S(2)}) copy-start(f32[1280]{0:T(1024)} %param.23) | copy-start | bytes 15364
  272.7 148.5 %all-to-all-start.4 = ((bf16[32,40,640]{2,1,0:T(8,128)(2,1)}), bf16[32,40,640]{2,1,0:T(8,128)(2,1)}, u32[]{:S(2)}, u32[]{:S(2)}) async-start(bf16[32,40,640]{2,1,0:T(8,128)(2,1)} %broadcast_in_dim.37), calls=%async_computation.4 | async-start | bytes 3276800 | tf_op jit(solution)/shard_map/all_to_all | solution.py:21
  287.2 190.6 %reduce-scatter.3.cloned.1.call-start = ((), (), s32[]{:S(2)}) async-start(), calls=%async_computation.8 | async-start | bytes 4096000 | tf_op jit(solution)/shard_map/reduce_scatter | solution.py:31
  415.5 2.9 copy-start.1
  419.8 1.3 copy-start.16
  440.5 73.2 %copy-start.2 = (bf16[1280,160]{0,1:T(8,128)(2,1)S(1)}, bf16[1280,160]{0,1:T(8,128)(2,1)}, u32[]{:S(2)}) copy-start(bf16[1280,160]{0,1:T(8,128)(2,1)} %fusion.30) | copy-start | bytes 1228804
  440.5 73.2 %copy-start.15 = (f32[160]{0:T(256)S(1)}, f32[160]{0:T(256)}, u32[]{:S(2)}) copy-start(f32[160]{0:T(256)} %param.28) | copy-start | bytes 1924
  440.5 73.1 %reduce-scatter.5.cloned.1.call-start = ((), (), s32[]{:S(2)}) async-start(), calls=%async_computation.9 | async-start | bytes 1228800 | tf_op jit(solution)/shard_map/reduce_scatter | solution.py:31
Sparse Core Ops, SparseCore 0:
  60.0 99.6 all-gather.6
  440.6 37.1 reduce-scatter.2
Sparse Core Ops, SparseCore 1:
  209.7 107.4 all-gather.10
  319.6 95.8 all-gather.8
  477.9 35.7 reduce-scatter.4
